TPU v7x, 8 devices: a whole 2x2x1 slice. The times are simulated.
8 devices in a mesh: dp: 1 (over z), ep: 8 (over x, y, core).
Axes of the slice: x: 2, y: 2, z: 1, core: 2. Of those that a mesh axis runs over, the one named last changes fastest.
Arguments:
- x: bfloat16 [1, 8, 256, 3584], P('dp', 'ep')
- expert: int32 [1, 8, 256, 8], P('dp', 'ep')
- slot: int32 [1, 8, 256, 8], P('dp', 'ep')
- gate: float32 [1, 8, 256, 8], P('dp', 'ep')
- w_gate: bfloat16 [32, 3584, 2560], P('ep')
- w_up: bfloat16 [32, 3584, 2560], P('ep')
- w_down: bfloat16 [32, 2560, 3584], P('ep')
- s_gate: bfloat16 [3584, 20480], replicated
- s_up: bfloat16 [3584, 20480], replicated
- s_down: bfloat16 [20480, 3584], replicated
Outputs:
- y: bfloat16 [1, 8, 256, 3584], P('dp', 'ep')
All inputs are finite; a program needn't handle non-finite values.
Results may differ from a plain program's by a relative error of at most 0.009.
Values are sent between devices in bfloat16 or wider.
A program may use at most 2 GiB of HBM per device.

v0:
```python
import jax
import jax.numpy as jnp
from jax import lax
from jax.sharding import NamedSharding, PartitionSpec as P


def einsum(form, a, b):
    return jnp.einsum(form, a.astype(jnp.float32), b.astype(jnp.float32))


def for_all(x, s_gate, s_up, s_down):
    h = jax.nn.silu(einsum("...d,df->...f", x, s_gate)) * einsum("...d,df->...f", x, s_up)
    return einsum("...f,fd->...d", h.astype(jnp.bfloat16), s_down)


def solution(mesh):
    def placed(v, *spec):
        return lax.with_sharding_constraint(v, NamedSharding(mesh, P(*spec)))

    def step(x, expert, slot, gate, w_gate, w_up, w_down, s_gate, s_up, s_down):
        experts, (tokens, top) = w_gate.shape[0], expert.shape[2:]
        slots = 5 * tokens * top // (4 * experts)
        to_expert = jax.nn.one_hot(expert, experts, dtype=jnp.bfloat16)
        to_slot = jax.nn.one_hot(slot, slots, dtype=jnp.bfloat16)
        weighted = to_expert * gate[..., None].astype(jnp.bfloat16)
        dispatch = einsum("abtke,abtkc->abtec", to_expert, to_slot).astype(jnp.bfloat16)
        combine = einsum("abtke,abtkc->abtec", weighted, to_slot).astype(jnp.bfloat16)
        z = einsum("abtec,abtd->aebcd", dispatch, x).astype(jnp.bfloat16)
        z = placed(z, "dp", None, "ep", None, None)
        z = placed(z, "dp", "ep", None, None, None)
        h = jax.nn.silu(einsum("aebcd,edf->aebcf", z, w_gate))
        h = (h * einsum("aebcd,edf->aebcf", z, w_up)).astype(jnp.bfloat16)
        out = einsum("aebcf,efd->aebcd", h, w_down).astype(jnp.bfloat16)
        out = placed(out, "dp", "ep", None, None, None)
        out = placed(out, "dp", None, "ep", None, None)
        y = einsum("abtec,aebcd->abtd", combine, out)
        return (y + for_all(x, s_gate, s_up, s_down)).astype(jnp.bfloat16)

    return step
```

profile of v0, /device:TPU:0, one launch (start us, length us, event | category | flops | bytes accessed | tf_op | source)
XLA Modules:
  0.0 636.5 jit_solution(18315073057318024212)
XLA Ops:
  0.0 0.0 copy-start
  0.0 1.0 copy.11
  1.0 0.8 copy.9
  1.8 3.5 convolution_convert_fusion.2
  5.3 0.0 copy-done
  5.3 12.5 %convolution_convert_fusion = bf16[32,80,3584]{2,1,0:T(8,128)(2,1)} fusion(bf16[256,32,80]{2,1,0:T(8,128)(2,1)} %convolution_convert_fusion.2, bf16[1,1,256,3584]{3,2,1,0:T(8,128)(2,1)S(1)} %copy-done), kind=kOutput, calls=%fused_computation.24 | convolution fusion | flops 4706795520 | bytes 21495808 | tf_op jit(solution)/abtec,abtd->aebcd/dot_general | solution.py:8
  17.7 0.0 copy-start.1
  17.7 4.9 all-to-all-start
  22.6 0.0 copy-done.1
  22.6 0.1 copy.10
  22.8 3.9 convolution_convert_fusion.1
  26.7 63.2 %convolution_bitcast_fusion.1 = f32[1,256,20480]{2,1,0:T(8,128)} fusion(bf16[3584,20480]{1,0:T(8,128)(2,1)} %param.7, bf16[1,1,256,3584]{3,2,1,0:T(8,128)(2,1)S(1)} %copy-done), kind=kOutput, calls=%fused_computation.7 | convolution fusion | flops 37580963840 | bytes 169607168 | tf_op jit(solution)/...d,df->...f/dot_general | solution.py:8
  89.9 133.5 %all-to-all-done = bf16[1,8,4,1,80,3584]{5,4,2,3,0,1:T(8,128)(2,1)} async-done(((bf16[1,8,4,1,80,3584]{5,4,2,3,0,1:T(8,128)(2,1)}), bf16[1,8,4,1,80,3584]{5,4,2,3,0,1:T(8,128)(2,1)}, u32[]{:S(2)}, u32[]{:S(2)}) %all-to-all-start) | async-done | bytes 18350112 | tf_op jit(solution)/sharding_constraint;jit(solution)/sharding_constraint | solution.py:18
  223.4 59.2 %fusion.2 = f32[4,8,80,2560]{3,2,1,0:T(8,128)} fusion(bf16[4,3584,2560]{2,1,0:T(8,128)(2,1)} %param.5, bf16[1,8,4,1,80,3584]{5,4,2,3,0,1:T(8,128)(2,1)} %all-to-all-done), kind=kOutput, calls=%fused_computation.2 | convolution fusion | flops 46976204800 | bytes 117964800 | tf_op jit(solution)/aebcd,edf->aebcf/dot_general | solution.py:8
  282.6 58.7 %fusion.7 = bf16[1,4,8,80,2560]{4,3,2,1,0:T(8,128)(2,1)} fusion(f32[4,8,80,2560]{3,2,1,0:T(8,128)} %fusion.2, bf16[4,3584,2560]{2,1,0:T(8,128)(2,1)} %param.4, bf16[1,8,4,1,80,3584]{5,4,2,3,0,1:T(8,128)(2,1)} %all-to-all-done), kind=kOutput, calls=%fused_computation.10 | convolution fusion | flops 47015526400 | bytes 131072000 | tf_op jit(solution)/aebcd,edf->aebcf/dot_general | solution.py:8
  341.3 60.0 %convert_bitcast_fusion = bf16[1,4,8,1,80,3584]{5,4,2,1,3,0:T(8,128)(2,1)} fusion(bf16[4,2560,3584]{2,1,0:T(8,128)(2,1)} %param.6, bf16[1,4,8,80,2560]{4,3,2,1,0:T(8,128)(2,1)} %fusion.7), kind=kOutput, calls=%fused_computation.20 | convolution fusion | flops 46985379840 | bytes 104857600 | tf_op jit(solution)/aebcf,efd->aebcd/dot_general | solution.py:8
  401.2 15.7 %copy.15 = bf16[1,4,8,1,80,3584]{5,4,1,3,0,2:T(8,128)(2,1)} copy(bf16[1,4,8,1,80,3584]{5,4,2,1,3,0:T(8,128)(2,1)} %convert_bitcast_fusion) | data formatting | bytes 36700160 | tf_op jit(solution)/sharding_constraint;jit(solution)/sharding_constraint | solution.py:18
  417.0 4.6 all-to-all-start.1
  421.6 63.0 %fusion.72 = bf16[256,20480]{1,0:T(8,128)(2,1)} fusion(bf16[3584,20480]{1,0:T(8,128)(2,1)} %param.8, bf16[1,1,256,3584]{3,2,1,0:T(8,128)(2,1)S(1)} %copy-done, f32[1,256,20480]{2,1,0:T(8,128)} %convolution_bitcast_fusion.1), kind=kOutput, calls=%bitcast_fusion.clone.1 | convolution fusion | flops 37612421120 | bytes 180092928 | tf_op jit(solution)/...d,df->...f/dot_general | solution.py:8
  484.6 55.2 %fusion.49 = f32[256,3584]{1,0:T(8,128)} fusion(bf16[20480,3584]{1,0:T(8,128)(2,1)} %param.9, bf16[256,20480]{1,0:T(8,128)(2,1)} %fusion.72), kind=kOutput, calls=%fused_computation.50 | convolution fusion | flops 37580963840 | bytes 160956416 | tf_op jit(solution)/...f,fd->...d/dot_general | solution.py:8
  539.7 81.5 %all-to-all-done.1 = bf16[1,4,8,1,80,3584]{5,4,1,3,0,2:T(8,128)(2,1)} async-done(((bf16[1,4,8,1,80,3584]{5,4,1,3,0,2:T(8,128)(2,1)}), bf16[1,4,8,1,80,3584]{5,4,1,3,0,2:T(8,128)(2,1)}, u32[]{:S(2)}, u32[]{:S(2)}) %all-to-all-start.1) | async-done | bytes 18350112 | tf_op jit(solution)/sharding_constraint;jit(solution)/sharding_constraint | solution.py:18
  621.2 15.3 %fusion.28 = bf16[1,1,256,3584]{3,2,1,0:T(8,128)(2,1)} fusion(f32[256,3584]{1,0:T(8,128)} %fusion.49, bf16[32,80,3584]{2,1,0:T(8,128)(2,1)} %bitcast.38, bf16[256,32,80]{2,1,0:T(8,128)(2,1)} %convolution_convert_fusion.1), kind=kOutput, calls=%fused_computation.28 | convolution fusion | flops 4699455488 | bytes 25165824 | tf_op jit(solution)/abtec,aebcd->abtd/dot_general | solution.py:8
  (1 shorter events, 0.0 us)
Async XLA Ops:
  0.0 5.3 copy-start
  17.7 4.9 copy-start.1
  17.7 205.7 %all-to-all-start = ((bf16[1,8,4,1,80,3584]{5,4,2,3,0,1:T(8,128)(2,1)}), bf16[1,8,4,1,80,3584]{5,4,2,3,0,1:T(8,128)(2,1)}, u32[]{:S(2)}, u32[]{:S(2)}) async-start(bf16[1,8,4,1,80,3584]{5,4,2,3,0,1:T(8,128)(2,1)} %bitcast.165), calls=%async_computation | async-start | bytes 36700160 | tf_op jit(solution)/sharding_constraint;jit(solution)/sharding_constraint | solution.py:18
  417.0 204.3 %all-to-all-start.1 = ((bf16[1,4,8,1,80,3584]{5,4,1,3,0,2:T(8,128)(2,1)}), bf16[1,4,8,1,80,3584]{5,4,1,3,0,2:T(8,128)(2,1)}, u32[]{:S(2)}, u32[]{:S(2)}) async-start(bf16[1,4,8,1,80,3584]{5,4,1,3,0,2:T(8,128)(2,1)} %copy.15), calls=%async_computation.1 | async-start | bytes 36700160 | tf_op jit(solution)/sharding_constraint;jit(solution)/sharding_constraint | solution.py:18
where the time goes:
time: 637 us
  matrix products  394 us (62%)
  waiting for transfers between devices  215 us (34%)
  local copies, waits for them, and re-layouts  17.6 us (3%)
  starting transfers between devices  9.48 us (1%)
    dot_general x10, matrix products, einsum(): return jnp.einsum(form, a.astype(jnp.float32), b.astype(jnp.float32))  394 us
    another operation x2, waiting for transfers between devices, placed(): return lax.with_sharding_constraint(v, NamedSharding(mesh, P(*spec)))  215 us
    another operation x1, local copies, waits for them, and re-layouts, placed(): return lax.with_sharding_constraint(v, NamedSharding(mesh, P(*spec)))  15.7 us
  transfers between devices with their start and end apart: 2, of which 2 were waited for; matrix products, arithmetic and copies ran while one was open for 29% of the time, Pallas kernels for 0%

commit v1 on v0

v1 whole, which is shorter than its diff:
```python
import functools

import jax
import jax.numpy as jnp
from jax import lax
from jax.experimental import pallas as pl
from jax.experimental.pallas import tpu as pltpu
from jax.sharding import PartitionSpec as P

CW = 512
WIN = 96
CWIN = 128
VMEM = 66_500_000


def silu_mul(g, u):
    return (g * jax.nn.sigmoid(g) * u).astype(jnp.bfloat16)


def dot(a, b):
    return jnp.dot(a, b, preferred_element_type=jnp.float32)


FLIPS = ((0, 0, 0), (0, 1, 0), (1, 0, 0), (1, 1, 0), (0, 0, 1), (0, 1, 1), (1, 0, 1), (1, 1, 1))
CHUNKS = 4
HALVES = 6
ROWS = 3072


def member(flip):
    me = lax.axis_index("ep")
    x, y, c = lax.div(me, 4), lax.rem(lax.div(me, 2), 2), lax.rem(me, 2)
    fx, fy, fc = flip
    return (x + fx * (1 - 2 * x)) * 4 + (y + fy * (1 - 2 * y)) * 2 + c + fc * (1 - 2 * c)


def greet():
    barrier = pltpu.get_barrier_semaphore()
    for flip in FLIPS[1:]:
        pl.semaphore_signal(
            barrier, inc=1, device_id={"ep": member(flip)}, device_id_type=pl.DeviceIdType.MESH
        )
    pl.semaphore_wait(barrier, len(FLIPS) - 1)


def remote(src, dst, ssem, rsem, to):
    return pltpu.make_async_remote_copy(
        src_ref=src, dst_ref=dst, send_sem=ssem, recv_sem=rsem,
        device_id={"ep": to}, device_id_type=pl.DeviceIdType.MESH,
    )


def start_all(copies):
    for c in copies:
        c.start()


def wait_all(copies):
    for c in copies:
        c.wait()


class Shared:
    def __init__(self, lo, tiles, x, sg, su, sd, h, wb, wsem):
        self.lo, self.tiles, self.nd = lo, tiles, x.shape[1] // CW
        self.x, self.sg, self.su, self.sd, self.h, self.wb, self.wsem = x, sg, su, sd, h, wb, wsem
        self.parts = tiles * CW // ROWS

    def up(self, i, slot):
        c = pl.ds(pl.multiple_of(self.lo + i * CW, CW), CW)
        return [
            pltpu.make_async_copy(w.at[:, c], self.wb.at[2 * slot + k], self.wsem.at[2 * slot + k])
            for k, w in enumerate((self.sg, self.su))
        ]

    def down(self, j, r, slot):
        c = pl.ds(pl.multiple_of(j * CW, CW), CW)
        return pltpu.make_async_copy(
            self.sd.at[pl.ds(self.lo + r * ROWS, ROWS), c], self.wb.at[slot, pl.ds(0, ROWS)], self.wsem.at[slot]
        )

    def begin(self):
        for i in range(HALVES // 2):
            start_all(self.up(i, i))

    def run(self, store, up_hooks, down_hooks):
        ring, tiles, nd, parts, h, wb = HALVES // 2, self.tiles, self.nd, self.parts, self.h, self.wb

        def up(i, _):
            slot = lax.rem(i, ring)
            wait_all(self.up(i, slot))
            g = dot(self.x[...], wb[2 * slot])
            u = dot(self.x[...], wb[2 * slot + 1])
            h[:, pl.ds(pl.multiple_of(i * CW, CW), CW)] = silu_mul(g, u)

            @pl.when(i + ring < tiles)
            def _():
                start_all(self.up(i + ring, slot))

            for k in range(ring):
                @pl.when(i == tiles - ring + k)
                def _():
                    for n in (2 * k, 2 * k + 1):
                        self.down(n // parts, n % parts, n).start()

            for at, fn in up_hooks:
                pl.when(i == at)(fn)
            return 0

        lax.fori_loop(0, tiles, up, 0)
        deep = HALVES // parts

        def down(j, _):
            base = lax.rem(j, deep) * parts
            o = None
            for r in range(parts):
                self.down(j, r, base + r).wait()
                d = dot(h[:, r * ROWS:(r + 1) * ROWS], wb[base + r, 0:ROWS, :])
                o = d if o is None else o + d
            store(pl.ds(pl.multiple_of(j * CW, CW), CW), o)

            @pl.when(j + deep < nd)
            def _():
                for r in range(parts):
                    self.down(j + deep, r, base + r).start()

            for at, fn in down_hooks:
                pl.when(j == at)(fn)
            return 0

        lax.fori_loop(0, nd, down, 0)


def first_kernel(lo, tiles, x, dense, sg, su, sd, out, x_all, w_all, h, wb, wsem, lsem, ssem, rsem, sw, rw):
    tokens = x.shape[0]
    core = lax.rem(lax.axis_index("ep"), 2)
    size = tokens // CHUNKS
    part = lambda k: pl.ds(k * size, size)
    work = Shared(lo, tiles, x, sg, su, sd, h, wb, wsem)
    work.begin()
    keep = [
        pltpu.make_async_copy(x, x_all.at[0], lsem.at[0]),
        pltpu.make_async_copy(dense, w_all.at[0], lsem.at[1]),
    ]
    start_all(keep)
    greet()

    own = lambda p, k: remote(
        x.at[part(k)], x_all.at[p, part(k)], ssem.at[p, k], rsem.at[p, k], member(FLIPS[p])
    )
    diag_to = (1 - core) * member(FLIPS[1]) + core * member(FLIPS[2])
    diag = lambda k: remote(
        x_all.at[2 - core, part(k)], x_all.at[3, part(k)], ssem.at[3, k], rsem.at[3, k], diag_to
    )
    mate = lambda p, k: remote(
        x_all.at[p, part(k)], x_all.at[p + 4, part(k)], ssem.at[p + 4, k], rsem.at[p + 4, k], member(FLIPS[4])
    )
    small = [
        remote(dense, w_all.at[p], sw.at[p], rw.at[p], member(FLIPS[p])) for p in range(1, len(FLIPS))
    ]
    start_all(small)
    for k in range(CHUNKS):
        own(1, k).start()
        own(2, k).start()
    for k in range(CHUNKS):
        own(4, k).start()

    def arrived(k):
        own(1, k).wait_recv()
        own(2, k).wait_recv()
        diag(k).start()
        mate(1, k).start()
        mate(2, k).start()

    def around(k):
        diag(k).wait_recv()
        mate(3, k).start()

    up_hooks = [(6, lambda: arrived(0)), (10, lambda: arrived(1)), (14, lambda: arrived(2))]
    down_hooks = [
        (0, lambda: arrived(3)), (2, lambda: around(0)), (4, lambda: around(1)), (5, lambda: around(2)),
        (6, lambda: around(3)),
    ]

    def store(c, o):
        out[:, c] = o

    work.run(store, up_hooks, down_hooks)
    wait_all(keep)
    wait_all(small)
    for k in range(CHUNKS):
        own(1, k).wait_send()
        own(2, k).wait_send()
        diag(k).wait_send()
        own(4, k).wait()
        for p in (1, 2, 3):
            mate(p, k).wait()


def last_kernel(lo, tiles, x, ya, yb, base, sg, su, sd, out, h, wb, acc, tv, rb, dg, rxy,
                wsem, lsem, ysem, ssem, rsem, s2, r2):
    tokens, d = x.shape
    f32, bf16 = jnp.float32, jnp.bfloat16
    core = lax.rem(lax.axis_index("ep"), 2)
    size = tokens // CHUNKS
    part = lambda k: pl.ds(k * size, size)
    work = Shared(lo, tiles, x, sg, su, sd, h, wb, wsem)
    order = (3, 1, 2, 0)
    load = lambda p, k: pltpu.make_async_copy(ya.at[p, part(k)], tv.at[p, part(k)], ysem.at[p, k])
    for k in range(CHUNKS):
        load(3, k).start()
    work.begin()
    for p in order[1:]:
        for k in range(CHUNKS):
            load(p, k).start()
    basecopy = pltpu.make_async_copy(base, acc, lsem.at[0])
    basecopy.start()
    greet()

    swap = lambda p, k: remote(
        yb.at[p, part(k)], rb.at[p, part(k)], ssem.at[p, k], rsem.at[p, k], member(FLIPS[4])
    )
    for p in order:
        for k in range(CHUNKS):
            swap(p, k).start()

    to_y, to_x = member(FLIPS[1]), member(FLIPS[2])
    near = (1 - core) * to_x + core * to_y
    relay = (1 - core) * to_y + core * to_x
    direct, turned = 2 - core, 1 + core
    send0 = lambda k: remote(tv.at[3, part(k)], dg.at[part(k)], s2.at[0, k], r2.at[0, k], near)
    send1 = lambda k: remote(
        tv.at[direct, part(k)], rxy.at[direct - 1, part(k)], s2.at[direct, k], r2.at[direct, k], near
    )
    send2 = lambda k: remote(
        tv.at[turned, part(k)], rxy.at[turned - 1, part(k)], s2.at[turned, k], r2.at[turned, k], relay
    )

    def far(k):
        load(3, k).wait()
        swap(3, k).wait_recv()
        tv[3, part(k)] = (tv[3, part(k)].astype(f32) + rb[3, part(k)].astype(f32)).astype(bf16)
        send0(k).start()

    def straight(k):
        load(direct, k).wait()
        swap(direct, k).wait_recv()
        tv[direct, part(k)] = (tv[direct, part(k)].astype(f32) + rb[direct, part(k)].astype(f32)).astype(bf16)
        send1(k).start()

    def passed(k):
        load(turned, k).wait()
        swap(turned, k).wait_recv()
        send0(k).wait_recv()
        tv[turned, part(k)] = (
            tv[turned, part(k)].astype(f32) + rb[turned, part(k)].astype(f32) + dg[part(k)].astype(f32)
        ).astype(bf16)
        send2(k).start()

    def both(fn, *ks):
        def run():
            for k in ks:
                fn(k)
        return run

    up_hooks = [
        (0, both(far, 0, 1, 2, 3)), (2, both(straight, 0, 1, 2, 3)),
        (4, both(passed, 0)), (6, both(passed, 1)), (8, both(passed, 2)), (10, both(passed, 3)),
        (11, basecopy.wait),
    ]

    def store(c, o):
        acc[:, c] = acc[:, c] + o

    work.run(store, up_hooks, [])
    for k in range(CHUNKS):
        load(0, k).wait()
        swap(0, k).wait_recv()
        for q in (1, 2):
            remote(tv.at[q, part(k)], rxy.at[q - 1, part(k)], s2.at[q, k], r2.at[q, k], to_y).wait_recv()

        def rows(i, _, k=k):
            r = pl.ds(pl.multiple_of(k * size + i * 16, 16), 16)
            out[r, :] = (
                acc[r, :] + tv[0, r, :].astype(f32) + rb[0, r, :].astype(f32)
                + rxy[0, r, :].astype(f32) + rxy[1, r, :].astype(f32)
            ).astype(bf16)
            return 0

        lax.fori_loop(0, size // 16, rows, 0)
    for k in range(CHUNKS):
        for p in range(4):
            swap(p, k).wait_send()
        send0(k).wait_send()
        send1(k).wait_send()
        send2(k).wait_send()


ANY = pl.BlockSpec(memory_space=pl.ANY)
VM = pl.BlockSpec(memory_space=pltpu.VMEM)


def shared_cost(tokens, d, width):
    return pl.CostEstimate(
        flops=6 * tokens * d * width, bytes_accessed=6 * d * width, transcendentals=tokens * width
    )


def first(x, dense, sg, su, sd, lo, tiles):
    tokens, d = x.shape
    n = len(FLIPS)
    dma = pltpu.SemaphoreType.DMA
    return pl.pallas_call(
        functools.partial(first_kernel, lo, tiles),
        out_shape=(
            jax.ShapeDtypeStruct((tokens, d), jnp.float32),
            jax.ShapeDtypeStruct((n, tokens, d), x.dtype),
            jax.ShapeDtypeStruct((n, *dense.shape), dense.dtype),
        ),
        in_specs=[VM, VM, ANY, ANY, ANY],
        out_specs=(VM, ANY, ANY),
        scratch_shapes=[
            pltpu.VMEM((tokens, tiles * CW), jnp.bfloat16),
            pltpu.VMEM((HALVES, d, CW), jnp.bfloat16),
            dma((HALVES,)), dma((2,)), dma((n, CHUNKS)), dma((n, CHUNKS)), dma((n,)), dma((n,)),
        ],
        compiler_params=pltpu.CompilerParams(vmem_limit_bytes=VMEM, collective_id=0, has_side_effects=True),
        cost_estimate=shared_cost(tokens, d, tiles * CW),
        name="first",
    )(x, dense, sg, su, sd)


def last(x, ya, yb, base, sg, su, sd, lo, tiles):
    tokens, d = x.shape
    dma = pltpu.SemaphoreType.DMA
    bf16 = jnp.bfloat16
    return pl.pallas_call(
        functools.partial(last_kernel, lo, tiles),
        out_shape=jax.ShapeDtypeStruct((tokens, d), bf16),
        in_specs=[VM, ANY, ANY, ANY, ANY, ANY, ANY],
        out_specs=VM,
        scratch_shapes=[
            pltpu.VMEM((tokens, tiles * CW), bf16),
            pltpu.VMEM((HALVES, d, CW), bf16),
            pltpu.VMEM((tokens, d), jnp.float32),
            pltpu.VMEM((4, tokens, d), bf16),
            pltpu.VMEM((4, tokens, d), bf16),
            pltpu.VMEM((tokens, d), bf16),
            pltpu.VMEM((2, tokens, d), bf16),
            dma((HALVES,)), dma((1,)), dma((4, CHUNKS)), dma((4, CHUNKS)), dma((4, CHUNKS)),
            dma((3, CHUNKS)), dma((3, CHUNKS)),
        ],
        compiler_params=pltpu.CompilerParams(vmem_limit_bytes=VMEM, collective_id=1, has_side_effects=True),
        cost_estimate=shared_cost(tokens, d, tiles * CW),
        name="last",
    )(x, ya, yb, base, sg, su, sd)


UNITS = 4
UW = 256
UNIT_COST = 104
LEAST_COST = 960


def routed_kernel(lo, units, x_hbm, wt_ref, wg, wu, wd, sg, su, sd, ya, yb_hbm, z, h, wb, yb, hm, cmat,
                  pos_v, off_v, off_s, wsem, xsem, ysem, osem, usem):
    ne, d, ff = wg.shape
    members, tokens = x_hbm.shape[:2]
    nf, nd = ff // CW, d // CW
    gitems, ditems = nf * ne, nd * ne
    ring = 3
    f32, bf16, i32 = jnp.float32, jnp.bfloat16, jnp.int32

    def gcopy(i, slot):
        e, f = lax.rem(i, ne), lax.div(i, ne)
        c = pl.ds(pl.multiple_of(f * CW, CW), CW)
        return [
            pltpu.make_async_copy(w.at[e, :, c], wb.at[2 * slot + k], wsem.at[2 * slot + k])
            for k, w in enumerate((wg, wu))
        ]

    def dcopy(i, slot):
        e, f = lax.rem(i, ne), lax.div(i, ne)
        c = pl.ds(pl.multiple_of(f * CW, CW), CW)
        return [pltpu.make_async_copy(wd.at[e, :, c], wb.at[slot, pl.ds(0, ff)], wsem.at[slot])]

    def xcopy(s, b):
        return [
            pltpu.make_async_copy(x_hbm.at[s, :, pl.ds(c * CW, CW)], yb.at[b, c], xsem.at[b, c])
            for c in range(nd)
        ]

    def start(copies):
        for c in copies:
            c.start()

    def wait(copies):
        for c in copies:
            c.wait()

    start(xcopy(0, 0))
    start(xcopy(1, 1))
    start(gcopy(0, 0))

    rows = members * ne
    me = lax.axis_index("ep")
    w = jnp.concatenate([wt_ref[s, me] for s in range(members)], axis=0)
    mask = w != 0.0
    mb = jnp.where(mask, 1.0, 0.0).astype(bf16)
    a0 = lax.broadcasted_iota(i32, (tokens, tokens), 0)
    a1 = lax.broadcasted_iota(i32, (tokens, tokens), 1)
    rank = dot(mb, jnp.where(a0 <= a1, 1.0, 0.0).astype(bf16))
    b0 = lax.broadcasted_iota(i32, (rows, rows), 0)
    b1 = lax.broadcasted_iota(i32, (rows, rows), 1)
    earlier = (lax.rem(b0, ne) == lax.rem(b1, ne)) & (b1 < b0)
    before = jnp.sum(dot(jnp.where(earlier, 1.0, 0.0).astype(bf16), mb), axis=1, keepdims=True)
    count = jnp.sum(jnp.where(mask, 1.0, 0.0), axis=1, keepdims=True)
    pos = jnp.where(mask, before + rank - 1.0, -1.0)
    for s in range(members):
        pos_v[s, 0:ne, :] = pos[s * ne:(s + 1) * ne]
    lane = lax.broadcasted_iota(i32, (rows, 128), 1)
    total = jnp.zeros((rows, tokens), f32)
    for s in range(members):
        every = jnp.concatenate([wt_ref[s, m] for m in range(members)], axis=0)
        total += jnp.where(every != 0.0, 1.0, 0.0)
    total = jnp.sum(total, axis=1, keepdims=True)
    off_v[...] = jnp.where(lane == 0, before, jnp.where(lane == 1, before + count, total)).astype(i32)
    cp = pltpu.make_async_copy(off_v, off_s, osem)
    cp.start()
    zero = jnp.zeros((16, d), bf16)

    def clear(i, _):
        for e in range(ne):
            z[e, pl.ds(pl.multiple_of(i * 16, 16), 16), :] = zero
        return 0

    lax.fori_loop(0, z.shape[1] // 16, clear, 0)
    cp.wait()

    costs = []
    for m in range(members):
        c = 0
        for e in range(ne):
            c += lax.div(off_s[m * ne + e, 2] + 127, 128) * 128
        costs.append(jnp.maximum(c, LEAST_COST))

    def give(_, carry):
        cost, held = carry
        best, who = jnp.where(held[0] < UNITS, cost[0], 1 << 20), 0
        for m in range(1, members):
            c = jnp.where(held[m] < UNITS, cost[m], 1 << 20)
            who = jnp.where(c < best, m, who)
            best = jnp.minimum(c, best)
        return (
            [jnp.where(who == m, cost[m] + UNIT_COST, cost[m]) for m in range(members)],
            [jnp.where(who == m, held[m] + 1, held[m]) for m in range(members)],
        )

    _, held = lax.fori_loop(0, units, give, (costs, [jnp.int32(0)] * members))
    first_unit, mine = 0, 0
    for m in range(members):
        first_unit += jnp.where(m < me, held[m], 0)
        mine += jnp.where(m == me, held[m], 0)

    def unit_col(u):
        return pl.multiple_of(lo + lax.div(first_unit + u, 2) * UW, UW)

    def ucopy(u):
        return [
            pltpu.make_async_copy(
                w.at[:, pl.ds(unit_col(u), UW)], wb.at[2 + u, :, pl.ds(k * UW, UW)], usem.at[u, k]
            )
            for k, w in enumerate((sg, su))
        ]

    def vcopy(u, q, par):
        c = pl.ds(pl.multiple_of(q * CW, CW), CW)
        return pltpu.make_async_copy(
            sd.at[pl.ds(unit_col(u), UW), c],
            z.at[u, pl.ds(0, UW), pl.ds(pl.multiple_of((2 + par) * CW, CW), CW)],
            usem.at[u, par],
        )

    def for_units(fn):
        for u in range(UNITS):
            @pl.when(u < mine)
            def _():
                fn(u)

    for_units(lambda u: start(ucopy(u)))
    odd = lax.rem(first_unit + me, 2)

    def units_of(half):
        u0 = lax.rem(odd + half, 2)
        return u0, jnp.maximum(lax.div(mine - u0 + 1, 2), 0)

    def window(s, e):
        st = off_s[s * ne + e, 0]
        return pl.multiple_of(lax.div(st, 16) * 16, 16)

    both = jnp.concatenate([pos, w, jnp.zeros((128 - 2 * rows, tokens), f32)], axis=0).T
    cl = lax.broadcasted_iota(i32, (tokens, CWIN), 1)
    for s in range(members):
        for e in range(ne):
            k = s * ne + e
            rel = both[:, k:k + 1].astype(i32) - window(s, e)
            cmat[s, :, e * CWIN:(e + 1) * CWIN] = jnp.where(
                rel == cl, both[:, rows + k:rows + k + 1], 0.0
            ).astype(bf16)

    wl = lax.broadcasted_iota(i32, (WIN, tokens), 0)

    def dispatch(s, _):
        b = lax.rem(s, 2)
        wait(xcopy(s, b))
        w0 = [window(s, e) for e in range(ne)]
        oh = jnp.concatenate([
            jnp.where(pos_v[s, e:e + 1, :].astype(i32) - w0[e] == wl, 1.0, 0.0).astype(bf16)
            for e in range(ne)
        ], axis=0)
        for c in range(nd):
            got = dot(oh, yb[b, c]).astype(bf16)
            for e in range(ne):
                at = (e, pl.ds(w0[e], WIN), slice(c * CW, (c + 1) * CW))
                z[at] = z[at] + got[e * WIN:(e + 1) * WIN]

        u0, nu = units_of(lax.div(s, 4))

        def unit(k, _):
            u = u0 + 2 * k
            @pl.when(lax.rem(s, 4) == 0)
            def _():
                wait(ucopy(u))

            xs = jnp.concatenate([yb[b, c] for c in range(nd)], axis=1)
            gu = dot(xs, wb[2 + u])
            hm[u, lax.rem(s, 4)] = silu_mul(gu[:, :UW], gu[:, UW:])
            return 0

        lax.fori_loop(0, nu, unit, 0)

        @pl.when(s + 2 < members)
        def _():
            start(xcopy(s + 2, b))

        return 0

    lax.fori_loop(0, members, dispatch, 0)
    for i in range(1, ring):
        start(gcopy(i, i))

    def tiles(e, body):
        n = off_s[(members - 1) * ne + e, 1]
        full = lax.div(n + 127, 256)
        lax.fori_loop(0, full, lambda m, c: (body(pl.multiple_of(m * 256, 256), 256), c)[1], 0)

        @pl.when(n > full * 256)
        def _():
            body(pl.multiple_of(full * 256, 256), 128)

    def gstep(i, _):
        e, f = lax.rem(i, ne), lax.div(i, ne)
        slot = lax.rem(i, ring)
        wait(gcopy(i, slot))
        c = pl.ds(pl.multiple_of(f * CW, CW), CW)

        def body(m, size):
            zt = z[e, pl.ds(m, size), :]
            g = dot(zt, wb[2 * slot])
            u = dot(zt, wb[2 * slot + 1])
            h[e, pl.ds(m, size), c] = silu_mul(g, u)

        tiles(e, body)

        @pl.when(i + ring < gitems)
        def _():
            start(gcopy(i + ring, slot))

        return 0

    lax.fori_loop(0, gitems, gstep, 0)

    for i in range(2 * ring):
        start(dcopy(i, i))

    def ycopy(q, par):
        c = pl.ds(pl.multiple_of(q * CW, CW), CW)
        half = members // 2
        return [
            pltpu.make_async_copy(yb.at[par, pl.ds(k * half, half)], y.at[:, :, c], ysem.at[par, k])
            for k, y in enumerate((ya, yb_hbm))
        ]

    for_units(lambda u: vcopy(u, 0, 0).start())

    def dpair(q, _):
        par = lax.rem(q, 2)

        @pl.when(q + 1 < nd)
        def _():
            for_units(lambda u: vcopy(u, q + 1, 1 - par).start())

        oc = pl.ds(pl.multiple_of(par * CW, CW), CW)

        def estep(e, _):
            i = q * ne + e
            slot = lax.rem(i, 2 * ring)
            wait(dcopy(i, slot))

            def body(m, size):
                o = dot(h[e, pl.ds(m, size), :], wb[slot, 0:ff, :])
                z[e, pl.ds(m, size), oc] = o.astype(bf16)

            tiles(e, body)

            @pl.when(i + 2 * ring < ditems)
            def _():
                start(dcopy(i + 2 * ring, slot))

            return 0

        lax.fori_loop(0, ne, estep, 0)

        @pl.when(q >= 2)
        def _():
            wait(ycopy(q - 2, par))

        for_units(lambda u: vcopy(u, q, par).wait())
        vc = pl.ds(pl.multiple_of((2 + par) * CW, CW), CW)

        def two(k, _):
            u0, nu = units_of(lax.div(k, 2))
            for n in range(UNITS // 2 + 1):
                @pl.when(nu == n)
                def _():
                    for j in range(2):
                        s = 2 * k + j
                        left = [cmat[s]] + [hm[u0 + 2 * i, lax.rem(s, 4)] for i in range(n)]
                        right = [z[e, pl.ds(window(s, e), CWIN), oc] for e in range(ne)]
                        right += [z[u0 + 2 * i, 0:UW, vc] for i in range(n)]
                        yb[par, s] = dot(
                            jnp.concatenate(left, axis=1), jnp.concatenate(right, axis=0)
                        ).astype(bf16)
            return 0

        lax.fori_loop(0, members // 2, two, 0)
        start(ycopy(q, par))
        return 0

    lax.fori_loop(0, nd, dpair, 0)
    wait(ycopy(nd - 2, (nd - 2) % 2))
    wait(ycopy(nd - 1, (nd - 1) % 2))


def routed(x_all, wt, wg, wu, wd, sg, su, sd, lo, width):
    members, tokens, d = x_all.shape
    ne, _, ff = wg.shape
    rows = members * 80
    anyspec = pl.BlockSpec(memory_space=pl.ANY)
    vspec = pl.BlockSpec(memory_space=pltpu.VMEM)
    half = jax.ShapeDtypeStruct((members // 2, tokens, d), jnp.bfloat16)
    return pl.pallas_call(
        functools.partial(routed_kernel, lo, 2 * width // UW),
        out_shape=(half, half),
        in_specs=[anyspec, vspec] + [anyspec] * 6,
        out_specs=(anyspec, anyspec),
        scratch_shapes=[
            pltpu.VMEM((ne, rows + 48, d), jnp.bfloat16),
            pltpu.VMEM((ne, rows, ff), jnp.bfloat16),
            pltpu.VMEM((6, d, CW), jnp.bfloat16),
            pltpu.VMEM((2, members, tokens, CW), jnp.bfloat16),
            pltpu.VMEM((UNITS, 4, tokens, UW), jnp.bfloat16),
            pltpu.VMEM((members, tokens, ne * CWIN), jnp.bfloat16),
            pltpu.VMEM((members, 8, tokens), jnp.float32),
            pltpu.VMEM((members * ne, 128), jnp.int32),
            pltpu.SMEM((members * ne, 128), jnp.int32),
            pltpu.SemaphoreType.DMA((6,)),
            pltpu.SemaphoreType.DMA((2, d // CW)),
            pltpu.SemaphoreType.DMA((2, 2)),
            pltpu.SemaphoreType.DMA,
            pltpu.SemaphoreType.DMA((UNITS, 2)),
        ],
        compiler_params=pltpu.CompilerParams(vmem_limit_bytes=VMEM),
        cost_estimate=pl.CostEstimate(
            flops=6 * 1600 * d * ff, bytes_accessed=6 * ne * d * ff, transcendentals=1600 * ff
        ),
        name="routed",
    )(x_all, wt, wg, wu, wd, sg, su, sd)


def solution(mesh):
    members = mesh.shape["ep"]

    def body(x, expert, slot, gate, wg, wu, wd, sg, su, sd):
        tokens, top = expert.shape[2:]
        experts = wg.shape[0] * members
        slots = 5 * tokens * top // (4 * experts)
        x2 = x.reshape(tokens, x.shape[-1])
        f32, bf16 = jnp.float32, jnp.bfloat16

        g = jnp.where(slot < slots, gate.astype(bf16).astype(f32), 0.0).reshape(tokens, top)
        ids = expert.reshape(tokens, top)
        dense = jnp.sum(
            jnp.where(ids.T[:, None, :] == jnp.arange(experts)[None, :, None], g.T[:, None, :], 0.0), axis=0
        )
        acc, x_all, w_all = first(x2, dense, sg, su, sd, 0, 18)
        ya, yb = routed(x_all, w_all.reshape(members, members, -1, tokens), wg, wu, wd, sg, su, sd, 18 * CW, 4 * CW)
        y = last(x2, ya, yb, acc, sg, su, sd, 22 * CW, 18)
        return y.reshape(x.shape)

    a = P("dp", "ep", None, None)
    w = P("ep", None, None)
    s = P(None, None)
    return jax.shard_map(
        body, mesh=mesh, in_specs=(a, a, a, a, w, w, w, s, s, s), out_specs=a, check_vma=False
    )
```

time: 637 us -> 291 us (0.46)
  matrix products: 394 us -> 0 us
  Pallas kernels: 0 us -> 282 us
  waiting for transfers between devices: 215 us -> 0 us
  local copies, waits for them, and re-layouts: 17.6 us -> 4.57 us
  starting transfers between devices: 9.48 us -> 0 us
    dot_general x10 -> x0, matrix products: 394 us -> none  [einsum(): return jnp.einsum(form, a.astype(jnp.float32), b.astype(jnp.float32))]
    pallas_call x0 -> x3, Pallas kernels: none -> 282 us  [the longest x1 134 us: routed(): pl.pallas_call(functools.partial(routed_kernel, lo, 2 * width // UW), out...]
    another operation x2 -> x0, waiting for transfers between devices: 215 us -> none  [placed(): return lax.with_sharding_constraint(v, NamedSharding(mesh, P(*spec)))]
    another operation x1 -> x0, local copies, waits for them, and re-layouts: 15.7 us -> none  [placed(): return lax.with_sharding_constraint(v, NamedSharding(mesh, P(*spec)))]
    another operation x2 -> x0, starting transfers between devices: 9.48 us -> none  [placed(): return lax.with_sharding_constraint(v, NamedSharding(mesh, P(*spec)))]
  transfers between devices with their start and end apart: 2 -> 0, of which waited for: 2 -> 0; matrix products, arithmetic and copies ran while one was open for 29% -> 0% of each run, Pallas kernels for 0% -> 0%
where the time goes in v1:
time: 291 us; the launch traced here: 289 us
  Pallas kernels  282 us (97%)
  local copies, waits for them, and re-layouts  4.57 us (2%)
    pallas_call x1, Pallas kernels, routed(): pl.pallas_call(functools.partial(routed_kernel, lo, 2 * width // UW), out...  134 us
    pallas_call x1, Pallas kernels, last(): pl.pallas_call(functools.partial(last_kernel, lo, tiles), out_shape=jax.S...  75.2 us
    pallas_call x1, Pallas kernels, first(): pl.pallas_call(functools.partial(first_kernel, lo, tiles), out_shape=(jax...  73.2 us

profile of v1, /device:TPU:0, one launch (start us, length us, event | category | flops | bytes accessed | tf_op | source)
XLA Modules:
  0.0 289.1 jit_solution(2464179614168023026)
XLA Ops:
  0.0 0.7 select_bitcast_fusion
  0.7 1.3 select_reduce_fusion.dense
  2.1 73.2 %first.1 = (f32[256,3584]{1,0:T(8,128)}, bf16[8,256,3584]{2,1,0:T(8,128)(2,1)}, f32[8,32,256]{2,1,0:T(8,128)}) custom-call(bf16[256,3584]{1,0:T(8,128)(2,1)} %bitcast.9, f32[32,256]{1,0:T(8,128)} %select_reduce_fusion.dense, bf16[3584,20480]{1,0:T(8,128)(2,1)} %sg.5, bf16[3584,20480]{1,0:T(8,128)(2,1)} %su.5, bf16[20480,3584]{1,0:T(8,128)(2,1)} %sd.5), custom_call_target="tpu_custom_call" | custom-call | flops 50734301184 | bytes 198180864 | tf_op jit(solution)/shard_map/first/pallas_call | solution.py:313
  75.3 1.7 reshape.20.wt_ref
  77.0 134.0 %routed.1 = (bf16[4,256,3584]{2,1,0:T(8,128)(2,1)}, bf16[4,256,3584]{2,1,0:T(8,128)(2,1)}) custom-call(bf16[8,256,3584]{2,1,0:T(8,128)(2,1)} %get-tuple-element.10.x_hbm, f32[8,8,4,256]{3,2,1,0:T(4,128)} %reshape.20.wt_ref, bf16[4,3584,2560]{2,1,0:T(8,128)(2,1)} %wg.1, bf16[4,3584,2560]{2,1,0:T(8,128)(2,1)} %wu.1, bf16[4,2560,3584]{2,1,0:T(8,128)(2,1)} %wd.1, ...), custom_call_target="tpu_custom_call" | custom-call | flops 88080384000 | bytes 220200960 | tf_op jit(solution)/shard_map/routed/pallas_call | solution.py:662
  211.0 75.2 %last.1 = bf16[256,3584]{1,0:T(8,128)(2,1)} custom-call(bf16[256,3584]{1,0:T(8,128)(2,1)} %bitcast.10, bf16[4,256,3584]{2,1,0:T(8,128)(2,1)} %get-tuple-element.12.ya, bf16[4,256,3584]{2,1,0:T(8,128)(2,1)} %get-tuple-element.13.yb, f32[256,3584]{1,0:T(8,128)} %get-tuple-element.14.base, bf16[3584,20480]{1,0:T(8,128)(2,1)} %sg.5, bf16[3584,20480]{1,0:T(8,128)(2,1)} %su.5, ...), custom_call_target="tpu_custom_call" | custom-call | flops 50734301184 | bytes 198180864 | tf_op jit(solution)/shard_map/last/pallas_call | solution.py:337
  286.2 2.8 copy.12

commit v2 on v1

--- a/solution.py
+++ b/solution.py
@@ -10,7 +10,7 @@
 CW = 512
 WIN = 96
 CWIN = 128
-VMEM = 66_500_000
+VMEM = 67_043_328
 
 
 def silu_mul(g, u):
@@ -23,6 +23,7 @@
 
 FLIPS = ((0, 0, 0), (0, 1, 0), (1, 0, 0), (1, 1, 0), (0, 0, 1), (0, 1, 1), (1, 0, 1), (1, 1, 1))
 CHUNKS = 4
+EDGE = 18
 HALVES = 6
 ROWS = 3072
 
@@ -176,10 +177,9 @@
         diag(k).wait_recv()
         mate(3, k).start()
 
-    up_hooks = [(6, lambda: arrived(0)), (10, lambda: arrived(1)), (14, lambda: arrived(2))]
+    up_hooks = [(4, lambda: arrived(0)), (8, lambda: arrived(1)), (12, lambda: arrived(2)), (16, lambda: arrived(3))]
     down_hooks = [
-        (0, lambda: arrived(3)), (2, lambda: around(0)), (4, lambda: around(1)), (5, lambda: around(2)),
-        (6, lambda: around(3)),
+        (2, lambda: around(0)), (4, lambda: around(1)), (5, lambda: around(2)), (6, lambda: around(3)),
     ]
 
     def store(c, o):
@@ -263,10 +263,10 @@
                 fn(k)
         return run
 
+    both(far, 0, 1, 2, 3)()
     up_hooks = [
-        (0, both(far, 0, 1, 2, 3)), (2, both(straight, 0, 1, 2, 3)),
-        (4, both(passed, 0)), (6, both(passed, 1)), (8, both(passed, 2)), (10, both(passed, 3)),
-        (11, basecopy.wait),
+        (0, both(straight, 0, 1, 2, 3)), (3, both(passed, 0)), (5, both(passed, 1)), (7, both(passed, 2)),
+        (9, both(passed, 3)), (11, basecopy.wait),
     ]
 
     def store(c, o):
@@ -356,13 +356,14 @@
     )(x, ya, yb, base, sg, su, sd)
 
 
-UNITS = 4
+UNITS = 5
+BLOCKS = 3
 UW = 256
-UNIT_COST = 104
-LEAST_COST = 960
-
-
-def routed_kernel(lo, units, x_hbm, wt_ref, wg, wu, wd, sg, su, sd, ya, yb_hbm, z, h, wb, yb, hm, cmat,
+UNIT_COST = 140
+LEAST_COST = 880
+
+
+def routed_kernel(lo, units, x_hbm, wt_ref, wg, wu, wd, sg, su, sd, ya, yb_hbm, z, h, wb, yb, hm,
                   pos_v, off_v, off_s, wsem, xsem, ysem, osem, usem):
     ne, d, ff = wg.shape
     members, tokens = x_hbm.shape[:2]
@@ -462,51 +463,52 @@
         first_unit += jnp.where(m < me, held[m], 0)
         mine += jnp.where(m == me, held[m], 0)
 
-    def unit_col(u):
-        return pl.multiple_of(lo + lax.div(first_unit + u, 2) * UW, UW)
-
-    def ucopy(u):
+    block0 = lax.div(first_unit, 2)
+    blocks = jnp.where(mine > 0, lax.div(first_unit + mine + 1, 2) - block0, 0)
+
+    def block_col(b):
+        return pl.multiple_of(lo + (block0 + b) * UW, UW)
+
+    def ucopy(b):
         return [
             pltpu.make_async_copy(
-                w.at[:, pl.ds(unit_col(u), UW)], wb.at[2 + u, :, pl.ds(k * UW, UW)], usem.at[u, k]
+                w.at[:, pl.ds(block_col(b), UW)], wb.at[2 + b, :, pl.ds(k * UW, UW)], usem.at[b, k]
             )
             for k, w in enumerate((sg, su))
         ]
 
-    def vcopy(u, q, par):
+    def vcopy(b, q, par):
         c = pl.ds(pl.multiple_of(q * CW, CW), CW)
         return pltpu.make_async_copy(
-            sd.at[pl.ds(unit_col(u), UW), c],
-            z.at[u, pl.ds(0, UW), pl.ds(pl.multiple_of((2 + par) * CW, CW), CW)],
-            usem.at[u, par],
+            sd.at[pl.ds(block_col(b), UW), c],
+            z.at[b, pl.ds(0, UW), pl.ds(pl.multiple_of((2 + par) * CW, CW), CW)],
+            usem.at[b, par],
         )
 
-    def for_units(fn):
-        for u in range(UNITS):
-            @pl.when(u < mine)
+    def for_blocks(fn):
+        for b in range(BLOCKS):
+            @pl.when(b < blocks)
             def _():
-                fn(u)
-
-    for_units(lambda u: start(ucopy(u)))
-    odd = lax.rem(first_unit + me, 2)
-
-    def units_of(half):
-        u0 = lax.rem(odd + half, 2)
-        return u0, jnp.maximum(lax.div(mine - u0 + 1, 2), 0)
+                fn(b)
+
+    for_blocks(lambda b: start(ucopy(b)))
+
+    def blocks_of(half):
+        kind = lax.rem(half + me, 2)
+        b0 = lax.div(first_unit - kind + 1, 2)
+        return b0 - block0, lax.div(first_unit + mine - kind + 1, 2) - b0
 
     def window(s, e):
         st = off_s[s * ne + e, 0]
         return pl.multiple_of(lax.div(st, 16) * 16, 16)
 
-    both = jnp.concatenate([pos, w, jnp.zeros((128 - 2 * rows, tokens), f32)], axis=0).T
-    cl = lax.broadcasted_iota(i32, (tokens, CWIN), 1)
-    for s in range(members):
-        for e in range(ne):
-            k = s * ne + e
-            rel = both[:, k:k + 1].astype(i32) - window(s, e)
-            cmat[s, :, e * CWIN:(e + 1) * CWIN] = jnp.where(
-                rel == cl, both[:, rows + k:rows + k + 1], 0.0
-            ).astype(bf16)
+    def cmat(s):
+        row = pl.multiple_of(lax.rem(s, 2) * tokens, tokens) if not isinstance(s, int) else s % 2 * tokens
+        at = lax.div(s, 2) if not isinstance(s, int) else s // 2
+        return z.at[at, pl.ds(row, tokens), pl.ds(4 * CW, CW)]
+
+    def cwindow(s, e):
+        return pl.multiple_of(jnp.minimum(window(s, e), z.shape[1] - CWIN), 16)
 
     wl = lax.broadcasted_iota(i32, (WIN, tokens), 0)
 
@@ -524,20 +526,20 @@
                 at = (e, pl.ds(w0[e], WIN), slice(c * CW, (c + 1) * CW))
                 z[at] = z[at] + got[e * WIN:(e + 1) * WIN]
 
-        u0, nu = units_of(lax.div(s, 4))
+        @pl.when(s == 0)
+        def _():
+            for_blocks(lambda b: wait(ucopy(b)))
+
+        b0, nb = blocks_of(lax.div(s, 4))
 
         def unit(k, _):
-            u = u0 + 2 * k
-            @pl.when(lax.rem(s, 4) == 0)
-            def _():
-                wait(ucopy(u))
-
-            xs = jnp.concatenate([yb[b, c] for c in range(nd)], axis=1)
-            gu = dot(xs, wb[2 + u])
-            hm[u, lax.rem(s, 4)] = silu_mul(gu[:, :UW], gu[:, UW:])
+            gu = dot(yb[b, 0], wb[2 + b0 + k, 0:CW, :])
+            for c in range(1, nd):
+                gu += dot(yb[b, c], wb[2 + b0 + k, c * CW:(c + 1) * CW, :])
+            hm[b0 + k, s] = silu_mul(gu[:, :UW], gu[:, UW:])
             return 0
 
-        lax.fori_loop(0, nu, unit, 0)
+        lax.fori_loop(0, nb, unit, 0)
 
         @pl.when(s + 2 < members)
         def _():
@@ -551,24 +553,36 @@
 
     def tiles(e, body):
         n = off_s[(members - 1) * ne + e, 1]
-        full = lax.div(n + 127, 256)
+        most = h.shape[1]
+        full = jnp.where(n > 512, 0, lax.div(n + 127, 256))
         lax.fori_loop(0, full, lambda m, c: (body(pl.multiple_of(m * 256, 256), 256), c)[1], 0)
 
-        @pl.when(n > full * 256)
+        @pl.when((n > full * 256) & (n <= 512))
         def _():
             body(pl.multiple_of(full * 256, 256), 128)
+
+        @pl.when(n > 512)
+        def _():
+            body(0, most)
+
+    def kdot(a, b, m, size, c, step, k):
+        part = k // 2 if size > 256 else k
+        o = None
+        for j in range(0, k, part):
+            one = dot(a[pl.ds(m, size), j:j + part], b[j:j + part, c:c + step])
+            o = one if o is None else o + one
+        return o
 
     def gstep(i, _):
         e, f = lax.rem(i, ne), lax.div(i, ne)
         slot = lax.rem(i, ring)
         wait(gcopy(i, slot))
-        c = pl.ds(pl.multiple_of(f * CW, CW), CW)
-
         def body(m, size):
-            zt = z[e, pl.ds(m, size), :]
-            g = dot(zt, wb[2 * slot])
-            u = dot(zt, wb[2 * slot + 1])
-            h[e, pl.ds(m, size), c] = silu_mul(g, u)
+            step = 256 if size > 256 else CW
+            for c in range(0, CW, step):
+                g = kdot(z.at[e], wb.at[2 * slot], m, size, c, step, d)
+                u = kdot(z.at[e], wb.at[2 * slot + 1], m, size, c, step, d)
+                h[e, pl.ds(m, size), pl.ds(pl.multiple_of(f * CW + c, step), step)] = silu_mul(g, u)
 
         tiles(e, body)
 
@@ -576,12 +590,24 @@
         def _():
             start(gcopy(i + ring, slot))
 
+        @pl.when(i + ring >= gitems)
+        def _():
+            start(dcopy(2 * (i + ring - gitems), 2 * slot))
+            start(dcopy(2 * (i + ring - gitems) + 1, 2 * slot + 1))
+
         return 0
 
     lax.fori_loop(0, gitems, gstep, 0)
 
-    for i in range(2 * ring):
-        start(dcopy(i, i))
+    both = jnp.concatenate([pos, w, jnp.zeros((128 - 2 * rows, tokens), f32)], axis=0).T
+    cl = lax.broadcasted_iota(i32, (tokens, CWIN), 1)
+    for s in range(members):
+        for e in range(ne):
+            k = s * ne + e
+            rel = both[:, k:k + 1].astype(i32) - cwindow(s, e)
+            cmat(s)[:, e * CWIN:(e + 1) * CWIN] = jnp.where(
+                rel == cl, both[:, rows + k:rows + k + 1], 0.0
+            ).astype(bf16)
 
     def ycopy(q, par):
         c = pl.ds(pl.multiple_of(q * CW, CW), CW)
@@ -591,25 +617,27 @@
             for k, y in enumerate((ya, yb_hbm))
         ]
 
-    for_units(lambda u: vcopy(u, 0, 0).start())
+    for_blocks(lambda u: vcopy(u, 0, 0).start())
 
     def dpair(q, _):
         par = lax.rem(q, 2)
 
         @pl.when(q + 1 < nd)
         def _():
-            for_units(lambda u: vcopy(u, q + 1, 1 - par).start())
+            for_blocks(lambda u: vcopy(u, q + 1, 1 - par).start())
 
         oc = pl.ds(pl.multiple_of(par * CW, CW), CW)
 
         def estep(e, _):
             i = q * ne + e
-            slot = lax.rem(i, 2 * ring)
+            slot = lax.rem(i + 2 * gitems, 2 * ring)
             wait(dcopy(i, slot))
 
             def body(m, size):
-                o = dot(h[e, pl.ds(m, size), :], wb[slot, 0:ff, :])
-                z[e, pl.ds(m, size), oc] = o.astype(bf16)
+                step = 256 if size > 256 else CW
+                for c in range(0, CW, step):
+                    o = kdot(h.at[e], wb.at[slot], m, size, c, step, ff)
+                    z[e, pl.ds(m, size), pl.ds(pl.multiple_of(par * CW + c, step), step)] = o.astype(bf16)
 
             tiles(e, body)
 
@@ -625,22 +653,24 @@
         def _():
             wait(ycopy(q - 2, par))
 
-        for_units(lambda u: vcopy(u, q, par).wait())
+        for_blocks(lambda u: vcopy(u, q, par).wait())
         vc = pl.ds(pl.multiple_of((2 + par) * CW, CW), CW)
 
         def two(k, _):
-            u0, nu = units_of(lax.div(k, 2))
-            for n in range(UNITS // 2 + 1):
-                @pl.when(nu == n)
+            b0, nb = blocks_of(lax.div(k, 2))
+            for n in range(BLOCKS + 1):
+                @pl.when(nb == n)
                 def _():
                     for j in range(2):
                         s = 2 * k + j
-                        left = [cmat[s]] + [hm[u0 + 2 * i, lax.rem(s, 4)] for i in range(n)]
-                        right = [z[e, pl.ds(window(s, e), CWIN), oc] for e in range(ne)]
-                        right += [z[u0 + 2 * i, 0:UW, vc] for i in range(n)]
-                        yb[par, s] = dot(
-                            jnp.concatenate(left, axis=1), jnp.concatenate(right, axis=0)
-                        ).astype(bf16)
+                        o = None
+                        for e in range(0, ne, 2):
+                            rows2 = [z[e + i, pl.ds(cwindow(s, e + i), CWIN), oc] for i in range(2)]
+                            one = dot(cmat(s)[:, e * CWIN:(e + 2) * CWIN], jnp.concatenate(rows2, axis=0))
+                            o = one if o is None else o + one
+                        for i in range(n):
+                            o += dot(hm[b0 + i, s], z[b0 + i, 0:UW, vc])
+                        yb[par, s] = o.astype(bf16)
             return 0
 
         lax.fori_loop(0, members // 2, two, 0)
@@ -665,12 +695,11 @@
         in_specs=[anyspec, vspec] + [anyspec] * 6,
         out_specs=(anyspec, anyspec),
         scratch_shapes=[
-            pltpu.VMEM((ne, rows + 48, d), jnp.bfloat16),
+            pltpu.VMEM((ne, rows + 16, d), jnp.bfloat16),
             pltpu.VMEM((ne, rows, ff), jnp.bfloat16),
             pltpu.VMEM((6, d, CW), jnp.bfloat16),
             pltpu.VMEM((2, members, tokens, CW), jnp.bfloat16),
-            pltpu.VMEM((UNITS, 4, tokens, UW), jnp.bfloat16),
-            pltpu.VMEM((members, tokens, ne * CWIN), jnp.bfloat16),
+            pltpu.VMEM((BLOCKS, members, tokens, UW), jnp.bfloat16),
             pltpu.VMEM((members, 8, tokens), jnp.float32),
             pltpu.VMEM((members * ne, 128), jnp.int32),
             pltpu.SMEM((members * ne, 128), jnp.int32),
@@ -678,7 +707,7 @@
             pltpu.SemaphoreType.DMA((2, d // CW)),
             pltpu.SemaphoreType.DMA((2, 2)),
             pltpu.SemaphoreType.DMA,
-            pltpu.SemaphoreType.DMA((UNITS, 2)),
+            pltpu.SemaphoreType.DMA((BLOCKS, 2)),
         ],
         compiler_params=pltpu.CompilerParams(vmem_limit_bytes=VMEM),
         cost_estimate=pl.CostEstimate(
@@ -695,6 +724,7 @@
         tokens, top = expert.shape[2:]
         experts = wg.shape[0] * members
         slots = 5 * tokens * top // (4 * experts)
+        middle = sg.shape[1] - 2 * EDGE * CW
         x2 = x.reshape(tokens, x.shape[-1])
         f32, bf16 = jnp.float32, jnp.bfloat16
 
@@ -702,10 +732,10 @@
         ids = expert.reshape(tokens, top)
         dense = jnp.sum(
             jnp.where(ids.T[:, None, :] == jnp.arange(experts)[None, :, None], g.T[:, None, :], 0.0), axis=0
-        )
-        acc, x_all, w_all = first(x2, dense, sg, su, sd, 0, 18)
-        ya, yb = routed(x_all, w_all.reshape(members, members, -1, tokens), wg, wu, wd, sg, su, sd, 18 * CW, 4 * CW)
-        y = last(x2, ya, yb, acc, sg, su, sd, 22 * CW, 18)
+        ).reshape(members, -1, tokens)
+        acc, x_all, w_all = first(x2, dense, sg, su, sd, 0, EDGE)
+        ya, yb = routed(x_all, w_all, wg, wu, wd, sg, su, sd, EDGE * CW, middle)
+        y = last(x2, ya, yb, acc, sg, su, sd, EDGE * CW + middle, EDGE)
         return y.reshape(x.shape)
 
     a = P("dp", "ep", None, None)

time: 291 us -> 287 us (0.986)
    pallas_call x1, Pallas kernels: 134 us -> 121 us  [routed(): pl.pallas_call(functools.partial(routed_kernel, lo, 2 * width // UW), out...]
    pallas_call x1, Pallas kernels: 75.2 us -> 82.5 us  [last(): pl.pallas_call(functools.partial(last_kernel, lo, tiles), out_shape=jax.S...]
    pallas_call x1, Pallas kernels: 73.2 us -> 77.2 us  [first(): pl.pallas_call(functools.partial(first_kernel, lo, tiles), out_shape=(jax...]
where the time goes in v2:
time: 287 us; the launch traced here: 286 us
  Pallas kernels  281 us (98%)
  local copies, waits for them, and re-layouts  3.47 us (1%)
    pallas_call x1, Pallas kernels, routed(): pl.pallas_call(functools.partial(routed_kernel, lo, 2 * width // UW), out...  121 us
    pallas_call x1, Pallas kernels, last(): pl.pallas_call(functools.partial(last_kernel, lo, tiles), out_shape=jax.S...  82.5 us
    pallas_call x1, Pallas kernels, first(): pl.pallas_call(functools.partial(first_kernel, lo, tiles), out_shape=(jax...  77.2 us

profile of v2, /device:TPU:0, one launch (start us, length us, event | category | flops | bytes accessed | tf_op | source)
XLA Modules:
  0.0 285.8 jit_solution(259876526824320652)
XLA Ops:
  0.0 0.7 select_bitcast_fusion
  0.7 0.7 select_reduce_fusion
  1.4 0.6 reshape.20.dense
  2.1 77.2 %first.1 = (f32[256,3584]{1,0:T(8,128)}, bf16[8,256,3584]{2,1,0:T(8,128)(2,1)}, f32[8,8,4,256]{3,2,1,0:T(4,128)}) custom-call(bf16[256,3584]{1,0:T(8,128)(2,1)} %bitcast.9, f32[8,4,256]{2,1,0:T(4,128)} %reshape.20.dense, bf16[3584,20480]{1,0:T(8,128)(2,1)} %sg.5, bf16[3584,20480]{1,0:T(8,128)(2,1)} %su.5, bf16[20480,3584]{1,0:T(8,128)(2,1)} %sd.5), custom_call_target="tpu_custom_call" | custom-call | flops 50734301184 | bytes 198180864 | tf_op jit(solution)/shard_map/first/pallas_call | solution.py:313
  79.2 121.2 %routed.1 = (bf16[4,256,3584]{2,1,0:T(8,128)(2,1)}, bf16[4,256,3584]{2,1,0:T(8,128)(2,1)}) custom-call(bf16[8,256,3584]{2,1,0:T(8,128)(2,1)} %get-tuple-element.10.x_hbm, f32[8,8,4,256]{3,2,1,0:T(4,128)} %get-tuple-element.11.wt_ref, bf16[4,3584,2560]{2,1,0:T(8,128)(2,1)} %wg.1, bf16[4,3584,2560]{2,1,0:T(8,128)(2,1)} %wu.1, bf16[4,2560,3584]{2,1,0:T(8,128)(2,1)} %wd.1, ...), custom_call_target="tpu_custom_call" | custom-call | flops 88080384000 | bytes 220200960 | tf_op jit(solution)/shard_map/routed/pallas_call | solution.py:692
  200.4 82.5 %last.1 = bf16[256,3584]{1,0:T(8,128)(2,1)} custom-call(bf16[256,3584]{1,0:T(8,128)(2,1)} %bitcast.10, bf16[4,256,3584]{2,1,0:T(8,128)(2,1)} %get-tuple-element.12.ya, bf16[4,256,3584]{2,1,0:T(8,128)(2,1)} %get-tuple-element.13.yb, f32[256,3584]{1,0:T(8,128)} %get-tuple-element.14.base, bf16[3584,20480]{1,0:T(8,128)(2,1)} %sg.5, bf16[3584,20480]{1,0:T(8,128)(2,1)} %su.5, ...), custom_call_target="tpu_custom_call" | custom-call | flops 50734301184 | bytes 198180864 | tf_op jit(solution)/shard_map/last/pallas_call | solution.py:337
  282.9 2.8 copy.12
